TPU v7x, 32 devices: a whole 2x2x4 slice. The times are simulated.
32 devices in a mesh: tm: 8 (over y, x, core), batch: 4 (over z).
Axes of the slice: x: 2, y: 2, z: 4, core: 2. Of those that a mesh axis runs over, the one named last changes fastest.
Arguments:
- obs_feats: bfloat16 [16, 512, 2048], P('batch', 'tm'), may hold values from -6 to 6
- next_feats: bfloat16 [16, 512, 2048], P('batch', 'tm'), may hold values from -6 to 6
- online_w: float32 [2048, 2048], P(('tm', 'batch')), may hold values from -6 to 6
- target_w: float32 [2048, 2048], P(('tm', 'batch')), may hold values from -6 to 6
- log_decay: float32 [2048], replicated, may hold values from -1 to 0, as said below
- step_scale: float32 [16, 512], P('batch', 'tm'), may hold values from 0.5 to 2
- online_heads: float32 [2, 2048], replicated, may hold values from -6 to 6
- target_heads: float32 [2, 2048], replicated, may hold values from -6 to 6
- reward: float32 [16, 512], P('batch', 'tm'), may hold values from -6 to 6
- next_action_log_prob: float32 [16, 512], P('batch', 'tm'), may hold values from -3 to 1
- resets: int32 [16, 512], P('batch', 'tm'), may hold values 0 or 1
- horizon: int32 [16], P('batch'), may hold values from 1 to 8
- burn_in: int32 [16], P('batch'), may hold values from 0 to 64
Outputs:
- grad_w: float32 [2048, 2048], P(('tm', 'batch'))
- new_target: float32 [2048, 2048], P(('tm', 'batch'))
- returns: float32 [16, 512], P('batch', 'tm')
Inputs may be any that keep to these rules, and one draw needn't show every extreme that they name: `log_decay`: every entry is negative.
All inputs are finite; a program needn't handle non-finite values. No bound on the sum of `resets` on one device may be relied on, other than what follows from the above.
Results may differ from a plain program's by a relative error of at most 0.0059.
Values may be sent and summed in bfloat16 or wider, within the bound.
A program may use at most 128 MiB of HBM per device.

v0:
```python
import jax
import jax.numpy as jnp
from jax import lax
from jax.sharding import PartitionSpec as P

NMAX = 8


DISCOUNT = 0.99
ENTROPY_COEFF = 0.2
POLYAK_RATE = 0.005
STEP_SIZE = 0.1


def shifted_2(block, axis, distance):
    devices = range(lax.axis_size(axis))
    route = [(i - distance, i) for i in devices if i - distance in devices]
    return lax.ppermute(block, axis, route)


def affine(earlier, later):
    return (later[0] * earlier[0], later[0] * earlier[1] + later[1])


def silu_slope(values):
    sigma = jax.nn.sigmoid(values)
    return sigma * (1.0 + values * (1.0 - sigma))


def returns_from(ext_reward, ext_value, ext_keep, row_horizon, span):
    total = jnp.zeros((ext_reward.shape[0], span), jnp.float32)
    alive = jnp.ones((ext_reward.shape[0], span), jnp.float32)
    for offset in range(NMAX):
        inside = (row_horizon > offset)[:, None]
        total = total + jnp.where(
            inside, DISCOUNT**offset * alive * ext_reward[:, offset : offset + span], 0.0
        )
        alive = alive * ext_keep[:, offset + 1 : offset + 1 + span]
        finish = (row_horizon == offset + 1)[:, None]
        total = total + jnp.where(
            finish,
            DISCOUNT ** (offset + 1) * alive * ext_value[:, offset + 1 : offset + 1 + span],
            0.0,
        )
    return total


def place_pair(pieces):
    return (pieces[0], pieces[1])


def shards(
    obs_feats,
    next_feats,
    online_w,
    target_w,
    log_decay,
    step_scale,
    online_heads,
    target_heads,
    reward,
    next_action_log_prob,
    resets,
    horizon,
    burn_in,
):
    rows_b, span, width = obs_feats.shape
    hidden = online_w.shape[1]
    flat_obs = obs_feats.reshape(rows_b * span, width)
    flat_next = next_feats.reshape(rows_b * span, width)
    input_scale = width ** (-0.5)
    scale_head = hidden ** (-0.5)
    w_online = online_w.astype(jnp.bfloat16)
    w_target = target_w.astype(jnp.bfloat16)
    near_on, near_tg = (
        lax.all_gather(w_online, "batch", axis=0, tiled=True),
        lax.all_gather(w_target, "batch", axis=0, tiled=True),
    )
    full_on, full_tg = place_pair(
        (
            lax.all_gather(near_on, "tm", axis=0, tiled=True),
            lax.all_gather(near_tg, "tm", axis=0, tiled=True),
        )
    )
    proj_on = (
        jnp.dot(flat_obs, full_on, preferred_element_type=jnp.float32) * input_scale
    ).reshape(rows_b, span, hidden)
    proj_tg = (
        jnp.dot(flat_next, full_tg, preferred_element_type=jnp.float32) * input_scale
    ).reshape(rows_b, span, hidden)
    decay = jnp.exp(step_scale[:, :, None] * log_decay[None, None, :])
    keeping = 1.0 - resets.astype(jnp.float32)
    factor = decay * keeping[:, :, None]
    spread = jnp.sqrt(1.0 - decay * decay)
    prods, local_on = lax.associative_scan(affine, (factor, spread * proj_on), axis=1)
    local_tg = lax.associative_scan(affine, (factor, spread * proj_tg), axis=1)[1]
    total_decay = prods[:, -1]
    end_on = local_on[:, -1]
    end_tg = local_tg[:, -1]
    blank_state = jnp.zeros((rows_b, hidden), jnp.float32)

    def relay_step(index, states):
        moved_on = total_decay * states[0] + end_on
        moved_tg = total_decay * states[1] + end_tg
        return shifted_2((moved_on, moved_tg), "tm", 1)

    start_on, start_tg = lax.fori_loop(
        0, lax.axis_size("tm") - 1, relay_step, (blank_state, blank_state)
    )
    state_on = local_on + prods * start_on[:, None, :]
    state_tg = local_tg + prods * start_tg[:, None, :]
    q_on = (
        jnp.einsum(
            "bth,kh->btk", jax.nn.silu(state_on), online_heads, precision=lax.Precision.HIGHEST
        )
        * scale_head
    )
    target_quality = (
        jnp.einsum(
            "bth,kh->btk", jax.nn.silu(state_tg), target_heads, precision=lax.Precision.HIGHEST
        )
        * scale_head
    )
    soft_value = jnp.min(target_quality, axis=2) - ENTROPY_COEFF * next_action_log_prob
    after_reward, after_value, after_keep = shifted_2(
        (reward[:, :NMAX], soft_value[:, :NMAX], keeping[:, :NMAX]), "tm", -1
    )
    returns = returns_from(
        jnp.concatenate([reward, after_reward], axis=1),
        jnp.concatenate([soft_value, after_value], axis=1),
        jnp.concatenate([keeping, after_keep], axis=1),
        horizon,
        span,
    )
    positions = jnp.arange(span, dtype=jnp.int32) + lax.axis_index("tm") * span
    weight_mask = (positions[None, :] >= burn_in[:, None]).astype(jnp.float32)
    slope = weight_mask[:, :, None] * (q_on - returns[:, :, None])
    grad_y = (
        jnp.einsum("btk,kh->bth", slope, online_heads, precision=lax.Precision.HIGHEST) * scale_head
    )
    grad_h = grad_y * silu_slope(state_on)
    shifted = jnp.concatenate([factor[:, 1:], jnp.ones((rows_b, 1, hidden), jnp.float32)], axis=1)
    tail_prod, local_adj = lax.associative_scan(affine, (shifted, grad_h), reverse=True, axis=1)
    leaving = factor[:, 0] * local_adj[:, 0]

    def back_step(index, entering):
        return shifted_2(total_decay * entering + leaving, "tm", -1)

    incoming = lax.fori_loop(0, lax.axis_size("tm") - 1, back_step, blank_state)
    adjoint = local_adj + tail_prod * incoming[:, None, :]
    grad_u = (spread * adjoint).astype(jnp.bfloat16).reshape(rows_b * span, hidden)
    full_term = (
        lax.dot_general(
            flat_obs, grad_u, (((0,), (0,)), ((), ())), preferred_element_type=jnp.float32
        )
        * input_scale
    )
    summed_block = lax.psum_scatter(full_term, "tm", scatter_dimension=0, tiled=True)
    grad_w = lax.psum_scatter(summed_block, "batch", scatter_dimension=0, tiled=True)
    new_target = (1.0 - POLYAK_RATE) * target_w + POLYAK_RATE * (online_w - STEP_SIZE * grad_w)
    return (grad_w, new_target, returns)


def solution(mesh):
    return jax.shard_map(
        shards,
        mesh=mesh,
        in_specs=(
            P("batch", "tm", None),
            P("batch", "tm", None),
            P(("tm", "batch"), None),
            P(("tm", "batch"), None),
            P(),
            P("batch", "tm"),
            P(),
            P(),
            P("batch", "tm"),
            P("batch", "tm"),
            P("batch", "tm"),
            P("batch"),
            P("batch"),
        ),
        out_specs=(P(("tm", "batch"), None), P(("tm", "batch"), None), P("batch", "tm")),
        check_vma=False,
    )
```

profile of v0, /device:TPU:1, one launch (start us, length us, event | category | flops | bytes accessed | tf_op | source)
XLA Modules:
  0.0 1076.7 jit_solution(10728122296800196855)
XLA Ops:
  11.0 28.7 %all-gather.5.cloned.1.call-done = bf16[256,2048]{1,0:T(8,128)(2,1)} async-done(((bf16[64,2048]{1,0:T(8,128)(2,1)}), bf16[256,2048]{1,0:T(8,128)(2,1)}) %all-gather.5.cloned.1.call-update) | async-done | bytes 1048592 | tf_op jit(solution)/shard_map/all_gather | solution.py:76
  39.8 29.5 %all-gather.9.cloned.1.call-done = bf16[256,2048]{1,0:T(8,128)(2,1)} async-done(((bf16[64,2048]{1,0:T(8,128)(2,1)}), bf16[256,2048]{1,0:T(8,128)(2,1)}) %all-gather.9.cloned.1.call-update) | async-done | bytes 1048592 | tf_op jit(solution)/shard_map/all_gather | solution.py:77
  77.5 48.3 %all-gather.7.cloned.1.call-done = bf16[2048,2048]{1,0:T(8,128)(2,1)} async-done(((bf16[256,2048]{1,0:T(8,128)(2,1)}), bf16[2048,2048]{1,0:T(8,128)(2,1)}) %all-gather.7.cloned.1.call-update) | async-done | bytes 8388624 | tf_op jit(solution)/shard_map/all_gather | solution.py:81
  125.8 7.1 convolution_multiply_fusion.2
  132.9 48.9 %all-gather.11.cloned.1.call-done = bf16[2048,2048]{1,0:T(8,128)(2,1)} async-done(((bf16[256,2048]{1,0:T(8,128)(2,1)}), bf16[2048,2048]{1,0:T(8,128)(2,1)}) %all-gather.11.cloned.1.call-update) | async-done | bytes 8388624 | tf_op jit(solution)/shard_map/all_gather | solution.py:82
  181.8 5.9 convolution_multiply_fusion.1
  196.7 5.4 slice.557
  202.1 5.4 slice.558
  207.5 5.4 slice.611
  212.9 5.4 slice.612
  315.1 5.5 slice.596
  320.6 5.5 slice.636
  331.6 5.4 slice.668
  337.0 5.4 slice.675
  342.4 5.4 slice.666
  510.3 53.1 %while.22 = (s32[]{:T(128)}, f32[4,2048]{1,0:T(4,128)S(1)}, f32[4,2048]{1,0:T(4,128)S(1)}, f32[4,2048]{1,0:T(4,128)S(1)}, f32[4,2048]{1,0:T(4,128)S(1)}, /*index=5*/f32[4,2048]{1,0:T(4,128)S(1)}, s32[]{:T(128)}) while((s32[]{:T(128)}, f32[4,2048]{1,0:T(4,128)S(1)}, f32[4,2048]{1,0:T(4,128)S(1)}, f32[4,2048]{1,0:T(4,128)S(1)}, ...), condition=%wide.region_1.0_spmd, body=%wide.region_0.0_spmd.sunk | while | flops 32770 | bytes 491677 | solution.py:107
  563.5 6.8 fusion.28
  574.4 9.1 slice.669
  583.7 8.9 slice.676
  592.6 9.0 slice.667
  610.4 5.4 slice.670
  615.8 5.4 slice.672
  621.1 8.9 slice.671
  630.1 8.9 slice.673
  703.7 5.4 slice.712
  710.1 9.0 slice.713
  828.6 9.6 rev.9
  838.2 5.7 rev.8
  843.9 40.5 %while.23 = (s32[]{:T(128)}, f32[4,2048]{1,0:T(4,128)S(1)}, f32[4,2048]{1,0:T(4,128)S(1)}, f32[4,2048]{1,0:T(4,128)S(1)}, s32[]{:T(128)}) while((s32[]{:T(128)}, f32[4,2048]{1,0:T(4,128)S(1)}, f32[4,2048]{1,0:T(4,128)S(1)}, f32[4,2048]{1,0:T(4,128)S(1)}, s32[]{:T(128)}) %tuple.128), condition=%wide.region_4.5_spmd, body=%wide.region_3.4_spmd.sunk | while | flops 16386 | bytes 262245 | solution.py:149
  884.5 11.3 %fusion = f32[2048,2048]{0,1:T(8,128)} fusion(bf16[4,64,2048]{2,1,0:T(8,128)(2,1)S(1)} %copy-done, f32[4,64,2048]{2,1,0:T(8,128)} %rev.8, f32[4,64,2048]{2,1,0:T(8,128)} %rev.9, f32[4,2048]{1,0:T(4,128)S(1)} %get-tuple-element.60, f32[2048]{0:T(1024)S(1)} %copy-done.68, f32[4,64]{1,0:T(4,128)S(1)} %copy-done.89), kind=kOutput, calls=%fused_computation.4 | convolution fusion | flops 2155347968 | bytes 22062080 | tf_op jit(solution)/shard_map/dot_general | solution.py:153
  895.8 120.0 %reduce-scatter.5.cloned.1.call-done = f32[256,2048]{0,1:T(8,128)} async-done(((f32[2048,2048]{0,1:T(8,128)}), f32[256,2048]{0,1:T(8,128)}) %reduce-scatter.5.cloned.1.call-update) | async-done | bytes 2097168 | tf_op jit(solution)/shard_map/reduce_scatter | solution.py:158
  1021.5 40.8 %reduce-scatter.7.cloned.1.call-done = f32[64,2048]{1,0:T(8,128)} async-done(((f32[256,2048]{1,0:T(8,128)}), f32[64,2048]{1,0:T(8,128)}) %reduce-scatter.7.cloned.1.call-update) | async-done | bytes 524304
  (497 shorter events, 579.5 us)
Async XLA Ops:
  7.2 118.6 %copy-start = (bf16[4,64,2048]{2,1,0:T(8,128)(2,1)S(1)}, bf16[4,64,2048]{2,1,0:T(8,128)(2,1)}, u32[]{:S(2)}) copy-start(bf16[4,64,2048]{2,1,0:T(8,128)(2,1)} %param.17) | copy-start | bytes 3145732
  7.2 67.3 %copy-start.90 = (s32[4]{0:T(128)S(1)}, s32[4]{0:T(128)}, u32[]{:S(2)}) copy-start(s32[4]{0:T(128)} %param.28) | copy-start | bytes 52
  7.2 32.6 %all-gather.5.cloned.1.call-start = ((), (), s32[]{:S(2)}) async-start(), calls=%async_computation.2 | async-start | bytes 1310720 | tf_op jit(solution)/shard_map/all_gather | solution.py:76
  9.1 60.2 %all-gather.9.cloned.1.call-start = ((), (), s32[]{:S(2)}) async-start(), calls=%async_computation.4 | async-start | bytes 1310720 | tf_op jit(solution)/shard_map/all_gather | solution.py:77
  11.0 114.8 %all-gather.7.cloned.1.call-start = ((), (), s32[]{:S(2)}) async-start(), calls=%async_computation.3 | async-start | bytes 9437184 | tf_op jit(solution)/shard_map/all_gather | solution.py:81
  39.8 142.0 %all-gather.11.cloned.1.call-start = ((), (), s32[]{:S(2)}) async-start(), calls=%async_computation.5 | async-start | bytes 9437184 | tf_op jit(solution)/shard_map/all_gather | solution.py:82
  69.3 946.5 %reduce-scatter.5.cloned.1.call-start = ((), (), s32[]{:S(2)}) async-start(), calls=%async_computation.6 | async-start | bytes 18874368 | tf_op jit(solution)/shard_map/reduce_scatter | solution.py:158
  69.4 5.8 collective-permute-start.3
  72.5 4.9 collective-permute-start.5
  510.3 5.4 collective-permute-start
  513.6 3.2 collective-permute-start.1
  516.8 6.2 collective-permute-start
  521.0 3.1 collective-permute-start.1
  524.1 6.0 collective-permute-start
  528.2 3.1 collective-permute-start.1
  531.3 6.9 collective-permute-start
  535.9 3.3 collective-permute-start.1
  539.2 7.1 collective-permute-start
  544.0 3.3 collective-permute-start.1
  547.3 7.1 collective-permute-start
  552.1 3.3 collective-permute-start.1
  555.4 7.1 collective-permute-start
  560.2 3.3 collective-permute-start.1
  570.3 31.3 %collective-permute-start.4 = (f32[4,8]{1,0:T(4,128)S(1)}, f32[4,8]{1,0:T(4,128)S(1)}, u32[]{:S(2)}, u32[]{:S(2)}) collective-permute-start(f32[4,8]{1,0:T(4,128)S(1)} %bitcast.118), channel_id=1, source_target_pairs={{4,0},{8,4},{12,8},{16,12},{20,16},{24,20},{28,24},{5,1},{9,5},{13... | collective-permute-start | bytes 392 | tf_op jit(solution)/shard_map/ppermute | solution.py:18
  843.9 6.4 collective-permute-start.2
  850.3 5.2 collective-permute-start.2
  855.6 5.2 collective-permute-start.2
  860.8 5.2 collective-permute-start.2
  866.1 6.1 collective-permute-start.2
  872.2 6.1 collective-permute-start.2
  878.3 6.1 collective-permute-start.2
  895.8 166.5 %reduce-scatter.7.cloned.1.call-start = ((), (), s32[]{:S(2)}) async-start(), calls=%async_computation.7 | async-start | bytes 2621440
  (93 other events, 1166.7 us)
Sparse Core Ops, SparseCore 0:
  10.2 29.5 all-gather.4
  41.9 27.3 all-gather.8
  71.2 54.5 all-gather.6
  127.5 54.2 all-gather.10
  895.9 119.8 reduce-scatter.4
  1018.9 43.3 reduce-scatter.6
where the time goes:
time: 1100 us; the launch traced here: 1080 us
  local copies, waits for them, and re-layouts  465 us (42%)
  waiting for transfers between devices  353 us (32%)
  other arithmetic  137 us (12%)
  starting transfers between devices  66.1 us (6%)
  matrix products  39.5 us (4%)
  between operations  15.7 us (1%)
    slice x41, local copies, waits for them, and re-layouts, shards(): lax.associative_scan(affine, (shifted, grad_h), reverse=True, axis=1)  138 us
    reduce_scatter x1, waiting for transfers between devices, shards(): lax.psum_scatter(full_term, 'tm', scatter_dimension=0, tiled=True)  120 us
    slice x36, local copies, waits for them, and re-layouts, shards(): lax.associative_scan(affine, (factor, spread * proj_on), axis=1)  82.1 us
    pad x20, local copies, waits for them, and re-layouts, shards(): lax.associative_scan(affine, (factor, spread * proj_on), axis=1)  69.8 us
    pad x20, local copies, waits for them, and re-layouts, shards(): lax.associative_scan(affine, (shifted, grad_h), reverse=True, axis=1)  67.1 us
    ppermute x24, starting transfers between devices, shifted_2(): return lax.ppermute(block, axis, route)  65.8 us
    all_gather x1, waiting for transfers between devices, shards(): lax.all_gather(near_tg, 'tm', axis=0, tiled=True)  48.9 us
    all_gather x1, waiting for transfers between devices, shards(): lax.all_gather(near_on, 'tm', axis=0, tiled=True)  48.3 us
  transfers between devices with their start and end apart: 30, of which 21 were waited for; matrix products, arithmetic and copies ran while one was open for 4% of the time, Pallas kernels for 0%

commit v1 on v0

v1 whole, which is shorter than its diff:
```python
import functools

import jax
import jax.numpy as jnp
from jax import lax
from jax.experimental import pallas as pl
from jax.experimental.pallas import tpu as pltpu
from jax.sharding import PartitionSpec as P

NMAX = 8
SUB = 8
HEADS = 2

DISCOUNT = 0.99
ENTROPY_COEFF = 0.2
POLYAK_RATE = 0.005
STEP_SIZE = 0.1


def returns_from(ext_reward, ext_value, ext_keep, row_horizon, span):
    total = jnp.zeros((ext_reward.shape[0], span), jnp.float32)
    alive = jnp.ones((ext_reward.shape[0], span), jnp.float32)
    for offset in range(NMAX):
        inside = (row_horizon > offset)[:, None]
        total = total + jnp.where(
            inside, DISCOUNT**offset * alive * ext_reward[:, offset : offset + span], 0.0
        )
        alive = alive * ext_keep[:, offset + 1 : offset + 1 + span]
        finish = (row_horizon == offset + 1)[:, None]
        total = total + jnp.where(
            finish,
            DISCOUNT ** (offset + 1) * alive * ext_value[:, offset + 1 : offset + 1 + span],
            0.0,
        )
    return total


def tile_scan(gain, value, place, reverse):
    for shift in (1, 2, 4):
        if reverse:
            inside, move = place < SUB - shift, SUB - shift
        else:
            inside, move = place >= shift, shift
        other_gain = jnp.where(inside, pltpu.roll(gain, move, 1), 1.0)
        other_value = jnp.where(inside, pltpu.roll(value, move, 1), 0.0)
        value = value + gain * other_value
        gain = gain * other_gain
    return gain, value


def forward_kernel(
    input_scale, x_ref, w_ref, factor_ref, spread_ref, heads_ref, q_ref, state_ref, carry_ref
):
    rows_b, block, width = x_ref.shape
    hid = w_ref.shape[1]

    @pl.when(pl.program_id(0) == 0)
    def _():
        carry_ref[...] = jnp.zeros_like(carry_ref)

    proj = jnp.dot(
        x_ref[...].reshape(rows_b * block, width), w_ref[...], preferred_element_type=jnp.float32
    )
    drive = (proj * input_scale).reshape(rows_b, block, hid) * spread_ref[...]
    place = lax.broadcasted_iota(jnp.int32, (rows_b, SUB, hid), 1)
    carry = carry_ref[...]
    for tile in range(block // SUB):
        at = slice(tile * SUB, (tile + 1) * SUB)
        gain, value = tile_scan(factor_ref[:, at, :], drive[:, at, :], place, False)
        state = value + gain * carry
        state_ref[:, at, :] = state
        carry = jnp.broadcast_to(state[:, SUB - 1 : SUB, :], state.shape)
    carry_ref[...] = carry
    state = state_ref[...].reshape(rows_b * block, hid)
    act = state / (1.0 + jnp.exp(-state))
    q_ref[0] = lax.dot_general(
        heads_ref[...],
        act,
        (((1,), (1,)), ((), ())),
        precision=lax.Precision.HIGHEST,
        preferred_element_type=jnp.float32,
    )


def backward_kernel(state_ref, after_ref, spread_ref, dq_ref, heads_ref, du_ref, carry_ref):
    rows_b, block, hid = state_ref.shape

    @pl.when(pl.program_id(0) == 0)
    def _():
        carry_ref[...] = jnp.zeros_like(carry_ref)

    grad_y = lax.dot_general(
        dq_ref[0],
        heads_ref[...],
        (((0,), (0,)), ((), ())),
        precision=lax.Precision.HIGHEST,
        preferred_element_type=jnp.float32,
    ).reshape(rows_b, block, hid)
    state = state_ref[...]
    sigma = 1.0 / (1.0 + jnp.exp(-state))
    grad_h = grad_y * (sigma * (1.0 + state * (1.0 - sigma)))
    place = lax.broadcasted_iota(jnp.int32, (rows_b, SUB, hid), 1)
    carry = carry_ref[...]
    pieces = [None] * (block // SUB)
    for tile in reversed(range(block // SUB)):
        at = slice(tile * SUB, (tile + 1) * SUB)
        gain, value = tile_scan(after_ref[:, at, :], grad_h[:, at, :], place, True)
        adjoint = value + gain * carry
        pieces[tile] = spread_ref[:, at, :] * adjoint
        carry = jnp.broadcast_to(adjoint[:, 0:1, :], adjoint.shape)
    carry_ref[...] = carry
    du_ref[...] = jnp.concatenate(pieces, axis=1).astype(jnp.bfloat16)


def forward(x, w, factor, spread, heads, block):
    rows_b, length, width = x.shape
    hid = w.shape[1]
    count = length // block
    whole = lambda j: (0, 0)
    part = lambda j: (0, j, 0)
    return pl.pallas_call(
        functools.partial(forward_kernel, width ** (-0.5)),
        grid=(count,),
        in_specs=[
            pl.BlockSpec((rows_b, block, width), part),
            pl.BlockSpec((width, hid), whole),
            pl.BlockSpec((rows_b, block, hid), part),
            pl.BlockSpec((rows_b, block, hid), part),
            pl.BlockSpec(heads.shape, whole),
        ],
        out_specs=[
            pl.BlockSpec((1, heads.shape[0], rows_b * block), lambda j: (j, 0, 0)),
            pl.BlockSpec((rows_b, block, hid), part),
        ],
        out_shape=[
            jax.ShapeDtypeStruct((count, heads.shape[0], rows_b * block), jnp.float32),
            jax.ShapeDtypeStruct((rows_b, length, hid), jnp.float32),
        ],
        scratch_shapes=[pltpu.VMEM((rows_b, SUB, hid), jnp.float32)],
        compiler_params=pltpu.CompilerParams(dimension_semantics=("arbitrary",)),
        cost_estimate=pl.CostEstimate(
            flops=2 * rows_b * length * width * hid,
            bytes_accessed=x.size * 2 + w.size * 2 + 3 * factor.size * 4,
            transcendentals=2 * factor.size,
        ),
    )(x, w, factor, spread, heads)


def backward(state, after, spread, dq, heads, block):
    rows_b, length, hid = state.shape
    count = length // block
    part = lambda j: (0, count - 1 - j, 0)
    return pl.pallas_call(
        backward_kernel,
        grid=(count,),
        in_specs=[
            pl.BlockSpec((rows_b, block, hid), part),
            pl.BlockSpec((rows_b, block, hid), part),
            pl.BlockSpec((rows_b, block, hid), part),
            pl.BlockSpec((1, heads.shape[0], rows_b * block), lambda j: (count - 1 - j, 0, 0)),
            pl.BlockSpec(heads.shape, lambda j: (0, 0)),
        ],
        out_specs=pl.BlockSpec((rows_b, block, hid), part),
        out_shape=jax.ShapeDtypeStruct((rows_b, length, hid), jnp.bfloat16),
        scratch_shapes=[pltpu.VMEM((rows_b, SUB, hid), jnp.float32)],
        compiler_params=pltpu.CompilerParams(dimension_semantics=("arbitrary",)),
        cost_estimate=pl.CostEstimate(
            flops=40 * state.size,
            bytes_accessed=3 * state.size * 4 + state.size * 2,
            transcendentals=2 * state.size,
        ),
    )(state, after, spread, dq, heads)


def shards(
    obs_feats,
    next_feats,
    online_w,
    target_w,
    log_decay,
    step_scale,
    online_heads,
    target_heads,
    reward,
    next_action_log_prob,
    resets,
    horizon,
    burn_in,
):
    rows_b, span, width = obs_feats.shape
    hidden = online_w.shape[1]
    n_tm, n_b = lax.axis_size("tm"), lax.axis_size("batch")
    length = span * n_tm
    hid = hidden // n_tm
    mine = lax.axis_index("tm")
    both = ("tm", "batch")
    block = span
    count = length // block
    scale_head = hidden ** (-0.5)
    local_rows = online_w.shape[0]

    small = jnp.stack([step_scale, 1.0 - resets.astype(jnp.float32), reward, next_action_log_prob])
    small = lax.all_gather(small, "tm", axis=2, tiled=True)
    weights = jnp.stack([online_w, target_w]).astype(jnp.bfloat16)
    weights = weights.reshape(2, local_rows, n_tm, hid).transpose(2, 0, 1, 3)
    weights = jnp.broadcast_to(
        weights[:, None], (n_tm, n_b, 2, local_rows, hid)
    ).reshape(n_tm * n_b, 2, local_rows, hid)
    weights = lax.all_to_all(weights, both, split_axis=0, concat_axis=0, tiled=True)
    w_on = weights[:, 0].reshape(width, hid)
    w_tg = weights[:, 1].reshape(width, hid)
    full_next = lax.all_gather(next_feats, "tm", axis=1, tiled=True)
    full_obs = lax.all_gather(obs_feats, "tm", axis=1, tiled=True)

    all_step, keeping, all_reward, all_log_prob = small[0], small[1], small[2], small[3]
    rates = lax.dynamic_slice_in_dim(log_decay, mine * hid, hid)
    decay = jnp.exp(all_step[:, :, None] * rates)
    factor = decay * keeping[:, :, None]
    spread = jnp.sqrt(1.0 - decay * decay)
    later = lambda v: jnp.concatenate([v[:, 1:], jnp.zeros_like(v[:, :1])], axis=1)
    after = jnp.exp(later(all_step)[:, :, None] * rates) * later(keeping)[:, :, None]

    pad_heads = lambda v: jnp.pad(
        lax.dynamic_slice_in_dim(v, mine * hid, hid, axis=1) * scale_head,
        ((0, SUB - HEADS), (0, 0)),
    )
    heads_on, heads_tg = pad_heads(online_heads), pad_heads(target_heads)

    part_tg, _ = forward(full_next, w_tg, factor, spread, heads_tg, block)
    part_on, state_on = forward(full_obs, w_on, factor, spread, heads_on, block)
    q_all = lax.psum(
        jnp.concatenate([part_on[:, :HEADS], part_tg[:, :HEADS]], axis=1), "tm"
    )
    q_all = (
        q_all.reshape(count, 2 * HEADS, rows_b, block)
        .transpose(1, 2, 0, 3)
        .reshape(2 * HEADS, rows_b, length)
    )
    soft_value = jnp.minimum(q_all[HEADS], q_all[HEADS + 1]) - ENTROPY_COEFF * all_log_prob
    padded = lambda v: jnp.pad(v, ((0, 0), (0, NMAX)))
    returns = returns_from(
        padded(all_reward), padded(soft_value), padded(keeping), horizon, length
    )
    positions = jnp.arange(length, dtype=jnp.int32)
    weight_mask = (positions[None, :] >= burn_in[:, None]).astype(jnp.float32)
    slope = weight_mask * (q_all[:HEADS] - returns[None])
    dq = jnp.pad(
        slope.reshape(HEADS, rows_b, count, block)
        .transpose(2, 0, 1, 3)
        .reshape(count, HEADS, rows_b * block),
        ((0, 0), (0, SUB - HEADS), (0, 0)),
    )
    grad_u = backward(state_on, after, spread, dq, heads_on, block)
    term = (
        lax.dot_general(
            full_obs.reshape(rows_b * length, width),
            grad_u.reshape(rows_b * length, hid),
            (((0,), (0,)), ((), ())),
            preferred_element_type=jnp.float32,
        )
        * (width ** (-0.5))
    ).astype(jnp.bfloat16)
    terms = lax.all_to_all(term, both, split_axis=0, concat_axis=0, tiled=True)
    terms = terms.reshape(n_tm, n_b, local_rows, hid).astype(jnp.float32)
    grad_w = terms.sum(axis=1).transpose(1, 0, 2).reshape(local_rows, hidden)
    new_target = (1.0 - POLYAK_RATE) * target_w + POLYAK_RATE * (online_w - STEP_SIZE * grad_w)
    return (grad_w, new_target, lax.dynamic_slice_in_dim(returns, mine * span, span, axis=1))


def solution(mesh):
    return jax.shard_map(
        shards,
        mesh=mesh,
        in_specs=(
            P("batch", "tm", None),
            P("batch", "tm", None),
            P(("tm", "batch"), None),
            P(("tm", "batch"), None),
            P(),
            P("batch", "tm"),
            P(),
            P(),
            P("batch", "tm"),
            P("batch", "tm"),
            P("batch", "tm"),
            P("batch"),
            P("batch"),
        ),
        out_specs=(P(("tm", "batch"), None), P(("tm", "batch"), None), P("batch", "tm")),
        check_vma=False,
    )
```

time: 1100 us -> 241 us (0.22); the launches traced: 1080 us -> 240 us
  local copies, waits for them, and re-layouts: 465 us -> 10.9 us
  waiting for transfers between devices: 353 us -> 90.9 us
  other arithmetic: 137 us -> 9.12 us
  blocking collectives: 0 us -> 58.6 us
  starting transfers between devices: 66.1 us -> 14.7 us
  Pallas kernels: 0 us -> 35.6 us
  matrix products: 39.5 us -> 6.06 us
    slice x96 -> x5, local copies, waits for them, and re-layouts: 260 us -> 3.3 us  [the longest x1 1.55 us: shards(): w_tg = weights[:, 1].reshape(width, hid)]
    pad x50 -> x3, local copies, waits for them, and re-layouts: 175 us -> 1.84 us  [the longest x2 1.21 us: shards(): jnp.pad(lax.dynamic_slice_in_dim(v, mine * hid, hid, axis=1) * scale_head...]
    reduce_scatter x1 -> x0, waiting for transfers between devices: 120 us -> none  [shards(): lax.psum_scatter(full_term, 'tm', scatter_dimension=0, tiled=True)]
    all_gather x4 -> x2, waiting for transfers between devices: 155 us -> 62.7 us  [the longest x1 42.2 us: shards(): full_obs = lax.all_gather(obs_feats, 'tm', axis=1, tiled=True)]
    add x55 -> x0, other arithmetic: 72.6 us -> none  [the longest x12 22.8 us: shards(): lax.associative_scan(affine, (shifted, grad_h), reverse=True, axis=1)]
    ppermute x24 -> x0, starting transfers between devices: 65.8 us -> none  [shifted_2(): return lax.ppermute(block, axis, route)]
    unnamed x7 -> x2, waiting for transfers between devices: 40.9 us -> 1.38 us
    all_gather x0 -> x1, blocking collectives: none -> 37.6 us  [shards(): small = lax.all_gather(small, 'tm', axis=2, tiled=True)]
  transfers between devices with their start and end apart: 30 -> 4, of which waited for: 21 -> 4; matrix products, arithmetic and copies ran while one was open for 4% -> 6% of each run, Pallas kernels for 0% -> 6%
where the time goes in v1:
time: 241 us; the launch traced here: 240 us
  waiting for transfers between devices  90.9 us (38%)
  blocking collectives  58.6 us (24%)
  Pallas kernels  35.6 us (15%)
  starting transfers between devices  14.7 us (6%)
  between operations  14.4 us (6%)
  local copies, waits for them, and re-layouts  10.9 us (5%)
  other arithmetic  9.12 us (4%)
  matrix products  6.06 us (3%)
    all_gather x1, waiting for transfers between devices, shards(): full_obs = lax.all_gather(obs_feats, 'tm', axis=1, tiled=True)  42.2 us
    all_gather x1, blocking collectives, shards(): small = lax.all_gather(small, 'tm', axis=2, tiled=True)  37.6 us
    pallas_call x2, Pallas kernels, forward(): pl.pallas_call(functools.partial(forward_kernel, width ** (-0.5)), grid=(...  27 us
    all_to_all x1, waiting for transfers between devices, shards(): terms = lax.all_to_all(term, both, split_axis=0, concat_axis=0, tiled=True)  25.7 us
    psum x1, blocking collectives, shards(): lax.psum(jnp.concatenate([part_on[:, :HEADS], part_tg[:, :HEADS]], axis=1...  21 us
    all_gather x1, waiting for transfers between devices, shards(): full_next = lax.all_gather(next_feats, 'tm', axis=1, tiled=True)  20.5 us
    pallas_call x1, Pallas kernels, backward(): pl.pallas_call(backward_kernel, grid=(count,), in_specs=[pl.BlockSpec((ro...  8.6 us
    all_to_all x1, starting transfers between devices, shards(): terms = lax.all_to_all(term, both, split_axis=0, concat_axis=0, tiled=True)  7.49 us
  transfers between devices with their start and end apart: 4, of which 4 were waited for; matrix products, arithmetic and copies ran while one was open for 6% of the time, Pallas kernels for 6%

profile of v1, /device:TPU:1, one launch (start us, length us, event | category | flops | bytes accessed | tf_op | source)
XLA Modules:
  0.0 240.3 jit_solution(6307624287505302143)
XLA Ops:
  7.2 0.7 all-gather.5.cloned.1.call-update
  8.0 0.7 all-gather.3.cloned.1.call-update
  9.1 1.6 broadcast_in_dim.132
  10.7 7.1 %all-to-all-start = ((bf16[32,2,64,256]{3,2,1,0:T(8,128)(2,1)}), bf16[32,2,64,256]{3,2,1,0:T(8,128)(2,1)S(1)}, u32[]{:S(2)}, u32[]{:S(2)}) async-start(bf16[32,2,64,256]{3,2,1,0:T(8,128)(2,1)} %bitcast.1), calls=%async_computation | async-start | bytes 4194304 | tf_op jit(solution)/shard_map/all_to_all | solution.py:209
  18.0 37.6 %all_gather.10 = f32[4,4,512]{1,0,2:T(4,128)S(1)} all-gather(f32[4,4,64]{1,0,2:T(4,128)S(1)} %copy.59), channel_id=1, replica_groups=mesh['tm'=8,'batch'=4] {'tm'}, dimensions={2}, use_global_device_ids=true | all-gather | bytes 36864 | tf_op jit(solution)/shard_map/all_gather | solution.py:203
  55.6 1.6 slice_multiply_fusion
  57.5 0.8 dynamic_slice.12
  58.3 0.7 dynamic-slice_multiply_fusion.1
  58.9 0.6 pad.23.heads_ref
  59.5 0.7 dynamic-slice_multiply_fusion
  60.2 0.6 pad.24.heads_ref
  61.2 3.7 %subtract_sqrt_fusion = (f32[4,512,256]{2,1,0:T(8,128)}, f32[4,512,256]{2,1,0:T(8,128)}, f32[4,512,256]{2,1,0:T(8,128)}) fusion(f32[256]{0:T(256)S(1)} %dynamic_slice.12, f32[4,512]{1,0:T(4,128)S(1)} %copy.60, f32[4,512]{1,0:T(4,128)S(1)} %copy.62, f32[4,512]{1,0:T(4,128)S(1)} %concatenate.12.clone, f32[4,512]{1,0:T(4,128)S(1)} %concatenate.11.clone), kind=kLoop, calls=%fused_computation.6 | loop fusion | flops 3145728 | bytes 6325248 | tf_op jit(solution)/shard_map/sqrt | solution.py:219
  65.0 1.2 all-to-all-done
  66.1 1.6 fusion.6
  67.7 20.5 %all-gather.5.cloned.1.call-done.x_ref = bf16[4,512,2048]{2,1,0:T(8,128)(2,1)} async-done(((bf16[4,64,2048]{2,1,0:T(8,128)(2,1)}), bf16[4,512,2048]{2,1,0:T(8,128)(2,1)}) %all-gather.5.cloned.1.call-update) | async-done | bytes 8388624 | tf_op jit(solution)/shard_map/all_gather | solution.py:212
  88.2 13.5 %shard_map.149 = (f32[8,8,256]{2,1,0:T(8,128)}, f32[4,512,256]{2,1,0:T(8,128)}) custom-call(bf16[4,512,2048]{2,1,0:T(8,128)(2,1)} %all-gather.5.cloned.1.call-done.x_ref, bf16[2048,256]{1,0:T(8,128)(2,1)} %bitcast.50, f32[4,512,256]{2,1,0:T(8,128)} %get-tuple-element.25.factor_ref, f32[4,512,256]{2,1,0:T(8,128)} %get-tuple-element.24.spread_ref, ...), custom_call_target="tpu_custom_call" | custom-call | flops 2147483648 | bytes 15728640 | tf_op jit(solution)/shard_map/pallas_call | solution.py:121
  101.7 0.8 slice.119
  102.5 42.2 %all-gather.3.cloned.1.call-done.x_ref = bf16[4,512,2048]{2,1,0:T(8,128)(2,1)} async-done(((bf16[4,64,2048]{2,1,0:T(8,128)(2,1)}), bf16[4,512,2048]{2,1,0:T(8,128)(2,1)}) %all-gather.3.cloned.1.call-update) | async-done | bytes 8388624 | tf_op jit(solution)/shard_map/all_gather | solution.py:213
  144.7 13.5 %shard_map.148 = (f32[8,8,256]{2,1,0:T(8,128)}, f32[4,512,256]{2,1,0:T(8,128)}) custom-call(bf16[4,512,2048]{2,1,0:T(8,128)(2,1)} %all-gather.3.cloned.1.call-done.x_ref, bf16[2048,256]{1,0:T(8,128)(2,1)} %bitcast.49, f32[4,512,256]{2,1,0:T(8,128)} %get-tuple-element.25.factor_ref, f32[4,512,256]{2,1,0:T(8,128)} %get-tuple-element.24.spread_ref, ...), custom_call_target="tpu_custom_call" | custom-call | flops 2147483648 | bytes 15728640 | tf_op jit(solution)/shard_map/pallas_call | solution.py:121
  158.3 0.8 slice.117
  159.2 21.0 %psum.7 = f32[4,4,8,64]{3,1,0,2:T(4,128)S(1)} all-reduce(f32[4,4,8,64]{3,1,0,2:T(4,128)S(1)} %bitcast.66), channel_id=1, replica_groups=mesh['tm'=8,'batch'=4] {'tm'}, use_global_device_ids=true, to_apply=%region_0.1 | all-reduce | flops 8192 | bytes 65536 | tf_op jit(solution)/shard_map/psum | solution.py:231
  180.3 0.1 copy.66
  180.5 1.0 select_add_fusion
  181.8 0.6 pad.28.dq_ref
  182.4 8.6 %shard_map.150 = bf16[4,512,256]{2,1,0:T(8,128)(2,1)} custom-call(f32[4,512,256]{2,1,0:T(8,128)} %get-tuple-element.6.state_ref, f32[4,512,256]{2,1,0:T(8,128)} %get-tuple-element.26.after_ref, f32[4,512,256]{2,1,0:T(8,128)} %get-tuple-element.24.spread_ref, f32[8,8,256]{2,1,0:T(8,128)} %pad.28.dq_ref, f32[8,256]{1,0:T(8,128)} %pad.23.heads_ref), custom_call_target="tpu_custom_call" | custom-call | flops 20971520 | bytes 7340032 | tf_op jit(solution)/shard_map/pallas_call | solution.py:153
  191.0 6.1 %fusion.2 = bf16[2048,256]{0,1:T(8,128)(2,1)S(1)} fusion(bf16[4,512,256]{2,1,0:T(8,128)(2,1)} %shard_map.150, bf16[4,512,2048]{2,1,0:T(8,128)(2,1)} %all-gather.3.cloned.1.call-done.x_ref), kind=kOutput, calls=%fused_computation.3 | convolution fusion | flops 2148532224 | bytes 10485760 | tf_op jit(solution)/shard_map/dot_general | solution.py:255
  197.1 1.3 copy.69
  198.4 7.5 %all-to-all-start.1 = ((bf16[32,64,256]{2,1,0:T(8,128)(2,1)}), bf16[32,64,256]{2,1,0:T(8,128)(2,1)S(1)}, u32[]{:S(2)}, u32[]{:S(2)}) async-start(bf16[32,64,256]{2,1,0:T(8,128)(2,1)} %bitcast.18), calls=%async_computation.1 | async-start | bytes 2097152 | tf_op jit(solution)/shard_map/all_to_all | solution.py:263
  205.9 0.7 copy.71
  206.6 25.7 %all-to-all-done.1 = bf16[32,64,256]{2,1,0:T(8,128)(2,1)S(1)} async-done(((bf16[32,64,256]{2,1,0:T(8,128)(2,1)}), bf16[32,64,256]{2,1,0:T(8,128)(2,1)S(1)}, u32[]{:S(2)}, u32[]{:S(2)}) %all-to-all-start.1) | async-done | bytes 1048608 | tf_op jit(solution)/shard_map/all_to_all | solution.py:263
  232.2 0.1 convert_reduce_fusion
  232.5 0.9 multiply_add_fusion
  (55 shorter events, 1.6 us)
Async XLA Ops:
  7.2 1.5 copy-start.1
  7.2 1.6 copy-start
  7.2 81.0 %all-gather.5.cloned.1.call-start = ((), (), s32[]{:S(2)}) async-start(), calls=%async_computation.3 | async-start | bytes 9437184 | tf_op jit(solution)/shard_map/all_gather | solution.py:212
  7.9 136.8 %all-gather.3.cloned.1.call-start = ((), (), s32[]{:S(2)}) async-start(), calls=%async_computation.2 | async-start | bytes 9437184 | tf_op jit(solution)/shard_map/all_gather | solution.py:213
  10.7 7.1 %copy-start.6 = (s32[4,64]{1,0:T(4,128)S(1)}, s32[4,64]{1,0:T(4,128)}, u32[]{:S(2)}) copy-start(s32[4,64]{1,0:T(4,128)} %param.23) | copy-start | bytes 3076
  10.7 7.1 %copy-start.7 = (f32[4,64]{1,0:T(4,128)S(1)}, f32[4,64]{1,0:T(4,128)}, u32[]{:S(2)}) copy-start(f32[4,64]{1,0:T(4,128)} %param.22) | copy-start | bytes 3076
  10.7 7.1 %copy-start.8 = (f32[4,64]{1,0:T(4,128)S(1)}, f32[4,64]{1,0:T(4,128)}, u32[]{:S(2)}) copy-start(f32[4,64]{1,0:T(4,128)} %param.21) | copy-start | bytes 3076
  10.7 7.2 %copy-start.9 = (f32[4,64]{1,0:T(4,128)S(1)}, f32[4,64]{1,0:T(4,128)}, u32[]{:S(2)}) copy-start(f32[4,64]{1,0:T(4,128)} %param.18) | copy-start | bytes 3076
  10.7 55.4 %all-to-all-start = ((bf16[32,2,64,256]{3,2,1,0:T(8,128)(2,1)}), bf16[32,2,64,256]{3,2,1,0:T(8,128)(2,1)S(1)}, u32[]{:S(2)}, u32[]{:S(2)}) async-start(bf16[32,2,64,256]{3,2,1,0:T(8,128)(2,1)} %bitcast.1), calls=%async_computation | async-start | bytes 4194304 | tf_op jit(solution)/shard_map/all_to_all | solution.py:209
  55.6 5.5 %copy-start.10 = (s32[4]{0:T(128)S(1)}, s32[4]{0:T(128)}, u32[]{:S(2)}) copy-start(s32[4]{0:T(128)} %param.24) | copy-start | bytes 52
  55.6 5.5 %copy-start.11 = (s32[4]{0:T(128)S(1)}, s32[4]{0:T(128)}, u32[]{:S(2)}) copy-start(s32[4]{0:T(128)} %param.25) | copy-start | bytes 52
  144.7 35.7 %copy-start.4 = (f32[1,4,512]{1,0,2:T(1,128)S(1)}, f32[1,4,512]{1,0,2:T(1,128)}, u32[]{:S(2)}) copy-start(f32[1,4,512]{1,0,2:T(1,128)} %get-tuple-element.20) | copy-start | bytes 24580
  144.7 35.8 %copy-start.5 = (f32[1,4,512]{1,0,2:T(1,128)S(1)}, f32[1,4,512]{1,0,2:T(1,128)}, u32[]{:S(2)}) copy-start(f32[1,4,512]{1,0,2:T(1,128)} %get-tuple-element.22) | copy-start | bytes 24580
  198.4 34.0 %copy-start.2 = (f32[64,2048]{1,0:T(8,128)S(1)}, f32[64,2048]{1,0:T(8,128)}, u32[]{:S(2)}) copy-start(f32[64,2048]{1,0:T(8,128)} %param.15) | copy-start | bytes 1572868
  198.4 33.8 %all-to-all-start.1 = ((bf16[32,64,256]{2,1,0:T(8,128)(2,1)}), bf16[32,64,256]{2,1,0:T(8,128)(2,1)S(1)}, u32[]{:S(2)}, u32[]{:S(2)}) async-start(bf16[32,64,256]{2,1,0:T(8,128)(2,1)} %bitcast.18), calls=%async_computation.1 | async-start | bytes 2097152 | tf_op jit(solution)/shard_map/all_to_all | solution.py:263
  232.4 1.0 copy-start.3
Sparse Core Ops, SparseCore 0:
  9.9 78.2 all-gather.4
  90.1 54.6 all-gather.2

commit v2 on v1

--- a/solution.py
+++ b/solution.py
@@ -170,6 +170,191 @@
             transcendentals=2 * state.size,
         ),
     )(state, after, spread, dq, heads)
+
+
+def ring_place(index, count):
+    if count & (count - 1):
+        return index, lambda p: p
+    place, shift = index, 1
+    while shift < count:
+        place = place ^ (index >> shift)
+        shift += 1
+    return place, lambda p: p ^ (p >> 1)
+
+
+def greet(peers):
+    barrier = pltpu.get_barrier_semaphore()
+    for peer in peers:
+        pl.semaphore_signal(
+            barrier, inc=1, device_id={"tm": peer}, device_id_type=pl.DeviceIdType.MESH
+        )
+    pl.semaphore_wait(barrier, len(peers))
+
+
+def gather_kernel(n, a_ref, b_ref, full_a, full_b, own_sem, out_sem, in_sem, pair_out, pair_in):
+    pairs = n // 2
+    me = lax.axis_index("tm")
+    lane = lax.rem(me, 2)
+    here, pair_at = ring_place(lax.div(me, 2), pairs)
+    device_at = lambda step: pair_at(lax.rem(here + step + pairs, pairs)) * 2 + lane
+    right, left, partner = device_at(1), device_at(-1), me + 1 - 2 * lane
+    greet((right, left, partner) if pairs > 1 else (partner,))
+    rows_b, span, _ = a_ref.shape
+
+    def slot(full, owner, rows):
+        return full.at[
+            pl.ds(rows[0], rows[1]), pl.ds(pl.multiple_of(owner * span, span), span), :
+        ]
+
+    def send(src, dst, peer, out, arrived):
+        copy = pltpu.make_async_remote_copy(
+            src_ref=src,
+            dst_ref=dst,
+            send_sem=out,
+            recv_sem=arrived,
+            device_id={"tm": peer},
+            device_id_type=pl.DeviceIdType.MESH,
+        )
+        copy.start()
+        return copy
+
+    whole, half = (0, rows_b), rows_b // 2
+    hops = pairs // 2
+    sources = ((a_ref, full_a), (b_ref, full_b))
+    pending, pair_copies, ring = [], [], {}
+
+    def rows_of(way, hop):
+        if 2 * hop < pairs:
+            return whole
+        return (0, half) if way == 0 else (half, rows_b - half)
+
+    def ring_send(which, way, hop):
+        rows = rows_of(way, hop)
+        if rows[1] == 0:
+            return
+        source, full = sources[which]
+        back = -1 if way == 0 else 1
+        owner = device_at(back * (hop - 1))
+        src = source.at[pl.ds(rows[0], rows[1])] if hop == 1 else slot(full, owner, rows)
+        ring[which, way, hop] = send(
+            src,
+            slot(full, owner, rows),
+            right if way == 0 else left,
+            out_sem.at[which, way, hop - 1],
+            in_sem.at[which, way, hop - 1],
+        )
+
+    def pair_send(which, src, owner, rows, index):
+        pair_copies.append(
+            send(
+                src,
+                slot(sources[which][1], owner, rows),
+                partner,
+                pair_out.at[which, index],
+                pair_in.at[which, index],
+            )
+        )
+
+    for which in range(2):
+        if hops:
+            ring_send(which, 0, 1)
+            ring_send(which, 1, 1)
+    for which in range(2):
+        source, full = sources[which]
+        pair_send(which, source, me, whole, 0)
+        own = pltpu.make_async_copy(source, slot(full, me, whole), own_sem.at[which])
+        own.start()
+        pending.append(own)
+    for hop in range(1, hops + 1):
+        for which in range(2):
+            for way in range(2):
+                if (which, way, hop) not in ring:
+                    continue
+                ring[which, way, hop].wait_recv()
+                if hop < hops:
+                    ring_send(which, way, hop + 1)
+                rows = rows_of(way, hop)
+                owner = device_at(-hop if way == 0 else hop)
+                block = slot(sources[which][1], owner, rows)
+                pair_send(which, block, owner, rows, 2 * hop - 1 + way)
+    for copy in ring.values():
+        copy.wait_send()
+    for copy in pair_copies:
+        copy.wait()
+    for own in pending:
+        own.wait()
+
+
+def gather_two(a, b, n):
+    rows_b, span, width = a.shape
+    full = jax.ShapeDtypeStruct((rows_b, span * n, width), a.dtype)
+    hops = max(n // 4, 1)
+    return pl.pallas_call(
+        functools.partial(gather_kernel, n),
+        out_shape=[full, full],
+        in_specs=[pl.BlockSpec(memory_space=pltpu.VMEM)] * 2,
+        out_specs=[pl.BlockSpec(memory_space=pl.ANY)] * 2,
+        scratch_shapes=[
+            pltpu.SemaphoreType.DMA((2,)),
+            pltpu.SemaphoreType.DMA((2, 2, hops)),
+            pltpu.SemaphoreType.DMA((2, 2, hops)),
+            pltpu.SemaphoreType.DMA((2, 2 * hops + 1)),
+            pltpu.SemaphoreType.DMA((2, 2 * hops + 1)),
+        ],
+        compiler_params=pltpu.CompilerParams(collective_id=1, has_side_effects=True),
+        cost_estimate=pl.CostEstimate(
+            flops=0, bytes_accessed=96 * n * rows_b * span * width, transcendentals=0
+        ),
+    )(a, b)
+
+
+def share_kernel(n, add, x_ref, o_ref, slots, send_sem, recv_sem):
+    me = lax.axis_index("tm")
+    peers = [lax.rem(me + step, n) for step in range(1, n)]
+    greet(peers)
+    copies = []
+    for step, peer in enumerate(peers):
+        copy = pltpu.make_async_remote_copy(
+            src_ref=x_ref,
+            dst_ref=slots.at[step] if add else o_ref.at[me],
+            send_sem=send_sem.at[step],
+            recv_sem=recv_sem.at[step],
+            device_id={"tm": peer},
+            device_id_type=pl.DeviceIdType.MESH,
+        )
+        copy.start()
+        copies.append(copy)
+    if not add:
+        o_ref[me] = x_ref[...]
+    for copy in copies:
+        copy.wait()
+    if add:
+        total = x_ref[...]
+        for step in range(n - 1):
+            total = total + slots[step]
+        o_ref[...] = total
+
+
+def share(x, n, add, collective_id):
+    shape = x.shape if add else (n,) + x.shape
+    slots = (n - 1,) + x.shape if add else (SUB, 128)
+    return pl.pallas_call(
+        functools.partial(share_kernel, n, add),
+        out_shape=jax.ShapeDtypeStruct(shape, x.dtype),
+        in_specs=[pl.BlockSpec(memory_space=pltpu.VMEM)],
+        out_specs=pl.BlockSpec(memory_space=pltpu.VMEM),
+        scratch_shapes=[
+            pltpu.VMEM(slots, x.dtype),
+            pltpu.SemaphoreType.DMA((n - 1,)),
+            pltpu.SemaphoreType.DMA((n - 1,)),
+        ],
+        compiler_params=pltpu.CompilerParams(
+            collective_id=collective_id, has_side_effects=True
+        ),
+        cost_estimate=pl.CostEstimate(
+            flops=x.size * n, bytes_accessed=x.size * 4 * n * 32, transcendentals=0
+        ),
+    )(x)
 
 
 def shards(
@@ -200,7 +385,8 @@
     local_rows = online_w.shape[0]
 
     small = jnp.stack([step_scale, 1.0 - resets.astype(jnp.float32), reward, next_action_log_prob])
-    small = lax.all_gather(small, "tm", axis=2, tiled=True)
+    small = share(small.reshape(4 * rows_b, span), n_tm, False, 0)
+    small = small.transpose(1, 0, 2).reshape(4, rows_b, length)
     weights = jnp.stack([online_w, target_w]).astype(jnp.bfloat16)
     weights = weights.reshape(2, local_rows, n_tm, hid).transpose(2, 0, 1, 3)
     weights = jnp.broadcast_to(
@@ -209,8 +395,7 @@
     weights = lax.all_to_all(weights, both, split_axis=0, concat_axis=0, tiled=True)
     w_on = weights[:, 0].reshape(width, hid)
     w_tg = weights[:, 1].reshape(width, hid)
-    full_next = lax.all_gather(next_feats, "tm", axis=1, tiled=True)
-    full_obs = lax.all_gather(obs_feats, "tm", axis=1, tiled=True)
+    full_next, full_obs = gather_two(next_feats, obs_feats, n_tm)
 
     all_step, keeping, all_reward, all_log_prob = small[0], small[1], small[2], small[3]
     rates = lax.dynamic_slice_in_dim(log_decay, mine * hid, hid)
@@ -228,8 +413,8 @@
 
     part_tg, _ = forward(full_next, w_tg, factor, spread, heads_tg, block)
     part_on, state_on = forward(full_obs, w_on, factor, spread, heads_on, block)
-    q_all = lax.psum(
-        jnp.concatenate([part_on[:, :HEADS], part_tg[:, :HEADS]], axis=1), "tm"
+    q_all = share(
+        jnp.concatenate([part_on[:, :HEADS], part_tg[:, :HEADS]], axis=1), n_tm, True, 2
     )
     q_all = (
         q_all.reshape(count, 2 * HEADS, rows_b, block)

time: 241 us -> 208 us (0.86)
  Pallas kernels: 35.6 us -> 141 us
  waiting for transfers between devices: 90.9 us -> 25.7 us
  blocking collectives: 58.6 us -> 0 us
  between operations: 14.4 us -> 0.91 us
  starting transfers between devices: 14.7 us -> 12.1 us
    pallas_call x0 -> x3, Pallas kernels: none -> 105 us  [the longest x1 80.9 us: gather_two(): pl.pallas_call(functools.partial(gather_kernel, n), out_shape=[full, full...]
    all_gather x2 -> x0, waiting for transfers between devices: 62.7 us -> none  [the longest x1 42.2 us: shards(): full_obs = lax.all_gather(obs_feats, 'tm', axis=1, tiled=True)]
    all_gather x1 -> x0, blocking collectives: 37.6 us -> none  [shards(): small = lax.all_gather(small, 'tm', axis=2, tiled=True)]
    psum x1 -> x0, blocking collectives: 21 us -> none  [shards(): lax.psum(jnp.concatenate([part_on[:, :HEADS], part_tg[:, :HEADS]], axis=1...]
    all_to_all x1, starting transfers between devices: 7.49 us -> 5 us  [shards(): terms = lax.all_to_all(term, both, split_axis=0, concat_axis=0, tiled=True)]
  transfers between devices with their start and end apart: 4 -> 2, of which waited for: 4 -> 1; matrix products, arithmetic and copies ran while one was open for 6% -> 4% of each run, Pallas kernels for 6% -> 47%
where the time goes in v2:
time: 208 us; the launch traced here: 207 us
  Pallas kernels  141 us (68%)
  waiting for transfers between devices  25.7 us (12%)
  starting transfers between devices  12.1 us (6%)
  other arithmetic  10 us (5%)
  local copies, waits for them, and re-layouts  10 us (5%)
  matrix products  7.17 us (3%)
    pallas_call x1, Pallas kernels, gather_two(): pl.pallas_call(functools.partial(gather_kernel, n), out_shape=[full, full...  80.9 us
    pallas_call x2, Pallas kernels, forward(): pl.pallas_call(functools.partial(forward_kernel, width ** (-0.5)), grid=(...  26.8 us
    all_to_all x1, waiting for transfers between devices, shards(): terms = lax.all_to_all(term, both, split_axis=0, concat_axis=0, tiled=True)  25.7 us
    pallas_call x2, Pallas kernels, share(): pl.pallas_call(functools.partial(share_kernel, n, add), out_shape=jax.Sha...  24.5 us
    pallas_call x1, Pallas kernels, backward(): pl.pallas_call(backward_kernel, grid=(count,), in_specs=[pl.BlockSpec((ro...  8.61 us
    dot_general x1, matrix products, shards(): lax.dot_general(full_obs.reshape(rows_b * length, width), grad_u.reshape(...  7.17 us
    all_to_all x1, starting transfers between devices, shards(): lax.all_to_all(weights, both, split_axis=0, concat_axis=0, tiled=True)  7.09 us
    all_to_all x1, starting transfers between devices, shards(): terms = lax.all_to_all(term, both, split_axis=0, concat_axis=0, tiled=True)  5 us
  transfers between devices with their start and end apart: 2, of which 1 were waited for; matrix products, arithmetic and copies ran while one was open for 4% of the time, Pallas kernels for 47%

profile of v2, /device:TPU:1, one launch (start us, length us, event | category | flops | bytes accessed | tf_op | source)
XLA Modules:
  0.0 206.7 jit_solution(7722052701034711559)
XLA Ops:
  0.6 1.1 convert.9
  1.8 1.1 convert.10
  3.0 0.1 copy.45
  3.1 1.6 broadcast_in_dim.132
  4.7 7.1 %all-to-all-start = ((bf16[32,2,64,256]{3,2,1,0:T(8,128)(2,1)}), bf16[32,2,64,256]{3,2,1,0:T(8,128)(2,1)S(1)}, u32[]{:S(2)}, u32[]{:S(2)}) async-start(bf16[32,2,64,256]{3,2,1,0:T(8,128)(2,1)} %bitcast.1), calls=%async_computation | async-start | bytes 4194304 | tf_op jit(solution)/shard_map/all_to_all | solution.py:395
  11.9 0.6 pad_maximum_fusion.1
  12.5 16.7 %shard_map.149 = f32[8,16,64]{2,1,0:T(8,128)} custom-call(f32[16,64]{1,0:T(8,128)} %bitcast.50), custom_call_target="tpu_custom_call" | custom-call | flops 8192 | bytes 1048576 | tf_op jit(solution)/shard_map/pallas_call | solution.py:341
  29.3 0.8 dynamic_slice.12
  30.0 0.7 dynamic-slice_multiply_fusion
  30.7 0.6 pad.24.heads_ref
  31.3 0.6 pad.23.heads_ref
  31.9 0.9 fusion.59
  33.2 80.9 %shard_map.148 = (bf16[4,512,2048]{2,1,0:T(8,128)(2,1)}, bf16[4,512,2048]{2,1,0:T(8,128)(2,1)}) custom-call(bf16[4,64,2048]{2,1,0:T(8,128)(2,1)} %a_ref.1, bf16[4,64,2048]{2,1,0:T(8,128)(2,1)} %b_ref.1), custom_call_target="tpu_custom_call" | custom-call | bytes 402653184 | tf_op jit(solution)/shard_map/pallas_call | solution.py:292
  114.3 3.6 %subtract_sqrt_fusion = (f32[4,512,256]{2,1,0:T(8,128)}, f32[4,512,256]{2,1,0:T(8,128)}, f32[4,512,256]{2,1,0:T(8,128)}) fusion(f32[256]{0:T(256)S(1)} %dynamic_slice.12, f32[4,512]{1,0:T(4,128)S(1)} %mul.203, f32[4,512]{1,0:T(4,128)S(1)} %mul.208, f32[4,512]{1,0:T(4,128)S(1)} %concatenate.12, f32[4,512]{1,0:T(4,128)S(1)} %concatenate.11), kind=kLoop, calls=%fused_computation.5 | loop fusion | flops 3145728 | bytes 6325248 | tf_op jit(solution)/shard_map/sqrt | solution.py:404
  117.9 1.5 fusion.58
  119.4 13.4 %shard_map.151 = (f32[8,8,256]{2,1,0:T(8,128)}, f32[4,512,256]{2,1,0:T(8,128)}) custom-call(bf16[4,512,2048]{2,1,0:T(8,128)(2,1)} %get-tuple-element.11.x_ref, bf16[2048,256]{1,0:T(8,128)(2,1)} %bitcast.39, f32[4,512,256]{2,1,0:T(8,128)} %get-tuple-element.20.factor_ref, f32[4,512,256]{2,1,0:T(8,128)} %get-tuple-element.19.spread_ref, f32[8,256]{1,0:T(8,128)} %pad.24.heads_ref), custom_call_target="tpu_custom_call" | custom-call | flops 2147483648 | bytes 15728640 | tf_op jit(solution)/shard_map/pallas_call | solution.py:121
  132.8 0.8 slice.123
  133.7 13.4 %shard_map.150 = (f32[8,8,256]{2,1,0:T(8,128)}, f32[4,512,256]{2,1,0:T(8,128)}) custom-call(bf16[4,512,2048]{2,1,0:T(8,128)(2,1)} %get-tuple-element.8.x_ref, bf16[2048,256]{1,0:T(8,128)(2,1)} %bitcast.38, f32[4,512,256]{2,1,0:T(8,128)} %get-tuple-element.20.factor_ref, f32[4,512,256]{2,1,0:T(8,128)} %get-tuple-element.19.spread_ref, f32[8,256]{1,0:T(8,128)} %pad.23.heads_ref), custom_call_target="tpu_custom_call" | custom-call | flops 2147483648 | bytes 15728640 | tf_op jit(solution)/shard_map/pallas_call | solution.py:121
  147.1 0.8 slice.121
  147.9 0.6 pad_maximum_fusion.x_ref
  148.6 7.7 %shard_map.152 = f32[8,4,256]{2,1,0:T(4,128)} custom-call(f32[8,4,256]{2,1,0:T(4,128)} %pad_maximum_fusion.x_ref), custom_call_target="tpu_custom_call" | custom-call | flops 65536 | bytes 8388608 | tf_op jit(solution)/shard_map/pallas_call | solution.py:341
  156.4 0.9 reshape.105
  157.4 0.2 fusion.15
  157.7 0.1 reshape.106
  157.7 0.6 pad.28.dq_ref
  158.4 8.6 %shard_map.153 = bf16[4,512,256]{2,1,0:T(8,128)(2,1)} custom-call(f32[4,512,256]{2,1,0:T(8,128)} %get-tuple-element.9.state_ref, f32[4,512,256]{2,1,0:T(8,128)} %get-tuple-element.21.after_ref, f32[4,512,256]{2,1,0:T(8,128)} %get-tuple-element.19.spread_ref, f32[8,8,256]{2,1,0:T(8,128)} %pad.28.dq_ref, f32[8,256]{1,0:T(8,128)} %pad.23.heads_ref), custom_call_target="tpu_custom_call" | custom-call | flops 20971520 | bytes 7340032 | tf_op jit(solution)/shard_map/pallas_call | solution.py:153
  167.0 7.2 %fusion.1 = bf16[2048,256]{1,0:T(8,128)(2,1)} fusion(bf16[4,512,2048]{2,1,0:T(8,128)(2,1)} %get-tuple-element.8.x_ref, bf16[4,512,256]{2,1,0:T(8,128)(2,1)} %shard_map.153), kind=kOutput, calls=%fused_computation.2 | convolution fusion | flops 2148532224 | bytes 10485760 | tf_op jit(solution)/shard_map/dot_general | solution.py:440
  174.2 5.0 %all-to-all-start.1 = ((bf16[32,64,256]{2,1,0:T(8,128)(2,1)}), bf16[32,64,256]{2,1,0:T(8,128)(2,1)S(1)}, u32[]{:S(2)}, u32[]{:S(2)}) async-start(bf16[32,64,256]{2,1,0:T(8,128)(2,1)} %bitcast.13), calls=%async_computation.1 | async-start | bytes 2097152 | tf_op jit(solution)/shard_map/all_to_all | solution.py:448
  179.2 0.7 constant_dynamic-slice_fusion
  179.8 25.7 %all-to-all-done.1 = bf16[32,64,256]{2,1,0:T(8,128)(2,1)S(1)} async-done(((bf16[32,64,256]{2,1,0:T(8,128)(2,1)}), bf16[32,64,256]{2,1,0:T(8,128)(2,1)S(1)}, u32[]{:S(2)}, u32[]{:S(2)}) %all-to-all-start.1) | async-done | bytes 1048608 | tf_op jit(solution)/shard_map/all_to_all | solution.py:448
  205.5 0.1 convert_reduce_fusion
  205.7 0.9 multiply_add_fusion
  (46 shorter events, 1.0 us)
Async XLA Ops:
  4.7 7.1 %copy-start.3 = (s32[4,64]{1,0:T(4,128)S(1)}, s32[4,64]{1,0:T(4,128)}, u32[]{:S(2)}) copy-start(s32[4,64]{1,0:T(4,128)} %param.23) | copy-start | bytes 3076
  4.7 7.2 %copy-start.4 = (f32[4,64]{1,0:T(4,128)S(1)}, f32[4,64]{1,0:T(4,128)}, u32[]{:S(2)}) copy-start(f32[4,64]{1,0:T(4,128)} %param.22) | copy-start | bytes 3076
  4.7 7.2 %copy-start.5 = (f32[4,64]{1,0:T(4,128)S(1)}, f32[4,64]{1,0:T(4,128)}, u32[]{:S(2)}) copy-start(f32[4,64]{1,0:T(4,128)} %param.21) | copy-start | bytes 3076
  4.7 7.2 %copy-start.6 = (f32[4,64]{1,0:T(4,128)S(1)}, f32[4,64]{1,0:T(4,128)}, u32[]{:S(2)}) copy-start(f32[4,64]{1,0:T(4,128)} %param.18) | copy-start | bytes 3076
  4.7 113.2 %all-to-all-start = ((bf16[32,2,64,256]{3,2,1,0:T(8,128)(2,1)}), bf16[32,2,64,256]{3,2,1,0:T(8,128)(2,1)S(1)}, u32[]{:S(2)}, u32[]{:S(2)}) async-start(bf16[32,2,64,256]{3,2,1,0:T(8,128)(2,1)} %bitcast.1), calls=%async_computation | async-start | bytes 4194304 | tf_op jit(solution)/shard_map/all_to_all | solution.py:395
  11.8 102.3 %copy-start.7 = (s32[4]{0:T(128)S(1)}, s32[4]{0:T(128)}, u32[]{:S(2)}) copy-start(s32[4]{0:T(128)} %param.24) | copy-start | bytes 52
  11.8 102.4 %copy-start.8 = (s32[4]{0:T(128)S(1)}, s32[4]{0:T(128)}, u32[]{:S(2)}) copy-start(s32[4]{0:T(128)} %param.25) | copy-start | bytes 52
  174.2 31.6 %copy-start = (f32[64,2048]{1,0:T(8,128)S(1)}, f32[64,2048]{1,0:T(8,128)}, u32[]{:S(2)}) copy-start(f32[64,2048]{1,0:T(8,128)} %param.16) | copy-start | bytes 1572868
  174.2 31.6 %copy-start.1 = (f32[64,2048]{1,0:T(8,128)S(1)}, f32[64,2048]{1,0:T(8,128)}, u32[]{:S(2)}) copy-start(f32[64,2048]{1,0:T(8,128)} %param.15) | copy-start | bytes 1572868
  174.2 31.3 %all-to-all-start.1 = ((bf16[32,64,256]{2,1,0:T(8,128)(2,1)}), bf16[32,64,256]{2,1,0:T(8,128)(2,1)S(1)}, u32[]{:S(2)}, u32[]{:S(2)}) async-start(bf16[32,64,256]{2,1,0:T(8,128)(2,1)} %bitcast.13), calls=%async_computation.1 | async-start | bytes 2097152 | tf_op jit(solution)/shard_map/all_to_all | solution.py:448
  205.7 1.0 copy-start.2

commit v3 on v2

--- a/solution.py
+++ b/solution.py
@@ -386,8 +386,9 @@
 
     small = jnp.stack([step_scale, 1.0 - resets.astype(jnp.float32), reward, next_action_log_prob])
     small = share(small.reshape(4 * rows_b, span), n_tm, False, 0)
+    online_in, target_in, small = lax.optimization_barrier((online_w, target_w, small))
     small = small.transpose(1, 0, 2).reshape(4, rows_b, length)
-    weights = jnp.stack([online_w, target_w]).astype(jnp.bfloat16)
+    weights = jnp.stack([online_in, target_in]).astype(jnp.bfloat16)
     weights = weights.reshape(2, local_rows, n_tm, hid).transpose(2, 0, 1, 3)
     weights = jnp.broadcast_to(
         weights[:, None], (n_tm, n_b, 2, local_rows, hid)

time: 208 us -> 209 us (level)
    pallas_call x1, Pallas kernels: 80.9 us -> 92.8 us  [gather_two(): pl.pallas_call(functools.partial(gather_kernel, n), out_shape=[full, full...]
    pallas_call x2, Pallas kernels: 24.5 us -> 15 us  [share(): pl.pallas_call(functools.partial(share_kernel, n, add), out_shape=jax.Sha...]
  transfers between devices with their start and end apart: 2 -> 2, of which waited for: 1 -> 1; matrix products, arithmetic and copies ran while one was open for 4% -> 4% of each run, Pallas kernels for 47% -> 45%
where the time goes in v3:
time: 209 us; the launch traced here: 208 us
  Pallas kernels  143 us (68%)
  waiting for transfers between devices  25.7 us (12%)
  starting transfers between devices  10.6 us (5%)
  other arithmetic  10.5 us (5%)
  local copies, waits for them, and re-layouts  9.97 us (5%)
  matrix products  7.19 us (3%)
    pallas_call x1, Pallas kernels, gather_two(): pl.pallas_call(functools.partial(gather_kernel, n), out_shape=[full, full...  92.8 us
    pallas_call x2, Pallas kernels, forward(): pl.pallas_call(functools.partial(forward_kernel, width ** (-0.5)), grid=(...  26.7 us
    all_to_all x1, waiting for transfers between devices, shards(): terms = lax.all_to_all(term, both, split_axis=0, concat_axis=0, tiled=True)  25.7 us
    pallas_call x2, Pallas kernels, share(): pl.pallas_call(functools.partial(share_kernel, n, add), out_shape=jax.Sha...  15 us
    pallas_call x1, Pallas kernels, backward(): pl.pallas_call(backward_kernel, grid=(count,), in_specs=[pl.BlockSpec((ro...  8.57 us
    dot_general x1, matrix products, shards(): lax.dot_general(full_obs.reshape(rows_b * length, width), grad_u.reshape(...  7.19 us
    all_to_all x1, starting transfers between devices, shards(): lax.all_to_all(weights, both, split_axis=0, concat_axis=0, tiled=True)  5.9 us
    all_to_all x1, starting transfers between devices, shards(): terms = lax.all_to_all(term, both, split_axis=0, concat_axis=0, tiled=True)  4.73 us
  transfers between devices with their start and end apart: 2, of which 1 were waited for; matrix products, arithmetic and copies ran while one was open for 4% of the time, Pallas kernels for 45%

profile of v3, /device:TPU:1, one launch (start us, length us, event | category | flops | bytes accessed | tf_op | source)
XLA Modules:
  0.0 207.9 jit_solution(633357024028235587)
XLA Ops:
  0.6 0.7 subtract_bitcast_fusion
  1.3 1.3 pad_maximum_fusion.1
  2.6 7.4 %shard_map.149 = f32[8,16,64]{2,1,0:T(8,128)} custom-call(f32[16,64]{1,0:T(8,128)} %bitcast.50), custom_call_target="tpu_custom_call" | custom-call | flops 8192 | bytes 1048576 | tf_op jit(solution)/shard_map/pallas_call | solution.py:341
  10.0 1.1 convert.9
  11.1 1.1 convert.10
  12.3 0.1 copy.45
  12.4 1.6 broadcast_in_dim.132
  14.0 5.9 %all-to-all-start = ((bf16[32,2,64,256]{3,2,1,0:T(8,128)(2,1)}), bf16[32,2,64,256]{3,2,1,0:T(8,128)(2,1)S(1)}, u32[]{:S(2)}, u32[]{:S(2)}) async-start(bf16[32,2,64,256]{3,2,1,0:T(8,128)(2,1)} %bitcast.6), calls=%async_computation | async-start | bytes 4194304 | tf_op jit(solution)/shard_map/all_to_all | solution.py:396
  20.0 0.8 dynamic_slice.12
  20.7 0.7 dynamic-slice_multiply_fusion
  21.4 0.6 pad.24.heads_ref
  22.0 0.6 pad.23.heads_ref
  23.1 92.8 %shard_map.148 = (bf16[4,512,2048]{2,1,0:T(8,128)(2,1)}, bf16[4,512,2048]{2,1,0:T(8,128)(2,1)}) custom-call(bf16[4,64,2048]{2,1,0:T(8,128)(2,1)} %a_ref.1, bf16[4,64,2048]{2,1,0:T(8,128)(2,1)} %b_ref.1), custom_call_target="tpu_custom_call" | custom-call | bytes 402653184 | tf_op jit(solution)/shard_map/pallas_call | solution.py:292
  116.0 3.6 %subtract_sqrt_fusion = (f32[4,512,256]{2,1,0:T(8,128)}, f32[4,512,256]{2,1,0:T(8,128)}, f32[4,512,256]{2,1,0:T(8,128)}) fusion(f32[256]{0:T(256)S(1)} %dynamic_slice.12, f32[4,512]{1,0:T(4,128)S(1)} %mul.203, f32[4,512]{1,0:T(4,128)S(1)} %mul.208, f32[4,512]{1,0:T(4,128)S(1)} %concatenate.12, f32[4,512]{1,0:T(4,128)S(1)} %concatenate.11), kind=kLoop, calls=%fused_computation.5 | loop fusion | flops 3145728 | bytes 6325248 | tf_op jit(solution)/shard_map/sqrt | solution.py:405
  119.6 1.5 fusion.58
  121.1 13.3 %shard_map.151 = (f32[8,8,256]{2,1,0:T(8,128)}, f32[4,512,256]{2,1,0:T(8,128)}) custom-call(bf16[4,512,2048]{2,1,0:T(8,128)(2,1)} %get-tuple-element.17.x_ref, bf16[2048,256]{1,0:T(8,128)(2,1)} %bitcast.39, f32[4,512,256]{2,1,0:T(8,128)} %get-tuple-element.26.factor_ref, f32[4,512,256]{2,1,0:T(8,128)} %get-tuple-element.25.spread_ref, f32[8,256]{1,0:T(8,128)} %pad.24.heads_ref), custom_call_target="tpu_custom_call" | custom-call | flops 2147483648 | bytes 15728640 | tf_op jit(solution)/shard_map/pallas_call | solution.py:121
  134.5 0.8 slice.123
  135.3 13.4 %shard_map.150 = (f32[8,8,256]{2,1,0:T(8,128)}, f32[4,512,256]{2,1,0:T(8,128)}) custom-call(bf16[4,512,2048]{2,1,0:T(8,128)(2,1)} %get-tuple-element.11.x_ref, bf16[2048,256]{1,0:T(8,128)(2,1)} %bitcast.38, f32[4,512,256]{2,1,0:T(8,128)} %get-tuple-element.26.factor_ref, f32[4,512,256]{2,1,0:T(8,128)} %get-tuple-element.25.spread_ref, f32[8,256]{1,0:T(8,128)} %pad.23.heads_ref), custom_call_target="tpu_custom_call" | custom-call | flops 2147483648 | bytes 15728640 | tf_op jit(solution)/shard_map/pallas_call | solution.py:121
  148.7 0.8 slice.121
  149.6 0.6 pad_maximum_fusion.x_ref
  150.3 7.6 %shard_map.152 = f32[8,4,256]{2,1,0:T(4,128)} custom-call(f32[8,4,256]{2,1,0:T(4,128)} %pad_maximum_fusion.x_ref), custom_call_target="tpu_custom_call" | custom-call | flops 65536 | bytes 8388608 | tf_op jit(solution)/shard_map/pallas_call | solution.py:341
  157.9 0.9 reshape.105
  158.9 0.2 fusion.15
  159.2 0.1 reshape.106
  159.3 0.6 pad.28.dq_ref
  159.9 8.6 %shard_map.153 = bf16[4,512,256]{2,1,0:T(8,128)(2,1)} custom-call(f32[4,512,256]{2,1,0:T(8,128)} %get-tuple-element.15.state_ref, f32[4,512,256]{2,1,0:T(8,128)} %get-tuple-element.27.after_ref, f32[4,512,256]{2,1,0:T(8,128)} %get-tuple-element.25.spread_ref, f32[8,8,256]{2,1,0:T(8,128)} %pad.28.dq_ref, f32[8,256]{1,0:T(8,128)} %pad.23.heads_ref), custom_call_target="tpu_custom_call" | custom-call | flops 20971520 | bytes 7340032 | tf_op jit(solution)/shard_map/pallas_call | solution.py:153
  168.5 7.2 %fusion.1 = bf16[2048,256]{1,0:T(8,128)(2,1)} fusion(bf16[4,512,2048]{2,1,0:T(8,128)(2,1)} %get-tuple-element.11.x_ref, bf16[4,512,256]{2,1,0:T(8,128)(2,1)} %shard_map.153), kind=kOutput, calls=%fused_computation.2 | convolution fusion | flops 2148532224 | bytes 10485760 | tf_op jit(solution)/shard_map/dot_general | solution.py:441
  175.7 4.7 %all-to-all-start.1 = ((bf16[32,64,256]{2,1,0:T(8,128)(2,1)}), bf16[32,64,256]{2,1,0:T(8,128)(2,1)S(1)}, u32[]{:S(2)}, u32[]{:S(2)}) async-start(bf16[32,64,256]{2,1,0:T(8,128)(2,1)} %bitcast.13), calls=%async_computation.1 | async-start | bytes 2097152 | tf_op jit(solution)/shard_map/all_to_all | solution.py:449
  180.4 0.7 constant_dynamic-slice_fusion
  181.1 25.7 %all-to-all-done.1 = bf16[32,64,256]{2,1,0:T(8,128)(2,1)S(1)} async-done(((bf16[32,64,256]{2,1,0:T(8,128)(2,1)}), bf16[32,64,256]{2,1,0:T(8,128)(2,1)S(1)}, u32[]{:S(2)}, u32[]{:S(2)}) %all-to-all-start.1) | async-done | bytes 1048608 | tf_op jit(solution)/shard_map/all_to_all | solution.py:449
  206.7 0.1 convert_reduce_fusion
  207.0 0.9 multiply_add_fusion
  (40 shorter events, 1.0 us)
Async XLA Ops:
  14.0 8.6 %copy-start.3 = (f32[8,16,64]{2,1,0:T(8,128)S(1)}, f32[8,16,64]{2,1,0:T(8,128)}, u32[]{:S(2)}) copy-start(f32[8,16,64]{2,1,0:T(8,128)} %shard_map.149) | copy-start | bytes 98308
  14.0 105.6 %all-to-all-start = ((bf16[32,2,64,256]{3,2,1,0:T(8,128)(2,1)}), bf16[32,2,64,256]{3,2,1,0:T(8,128)(2,1)S(1)}, u32[]{:S(2)}, u32[]{:S(2)}) async-start(bf16[32,2,64,256]{3,2,1,0:T(8,128)(2,1)} %bitcast.6), calls=%async_computation | async-start | bytes 4194304 | tf_op jit(solution)/shard_map/all_to_all | solution.py:396
  19.9 95.9 %copy-start.4 = (s32[4]{0:T(128)S(1)}, s32[4]{0:T(128)}, u32[]{:S(2)}) copy-start(s32[4]{0:T(128)} %param.24) | copy-start | bytes 52
  20.0 96.0 %copy-start.5 = (s32[4]{0:T(128)S(1)}, s32[4]{0:T(128)}, u32[]{:S(2)}) copy-start(s32[4]{0:T(128)} %param.25) | copy-start | bytes 52
  175.7 31.3 %copy-start = (f32[64,2048]{1,0:T(8,128)S(1)}, f32[64,2048]{1,0:T(8,128)}, u32[]{:S(2)}) copy-start(f32[64,2048]{1,0:T(8,128)} %param.16) | copy-start | bytes 1572868
  175.7 31.3 %copy-start.1 = (f32[64,2048]{1,0:T(8,128)S(1)}, f32[64,2048]{1,0:T(8,128)}, u32[]{:S(2)}) copy-start(f32[64,2048]{1,0:T(8,128)} %param.15) | copy-start | bytes 1572868
  175.7 31.1 %all-to-all-start.1 = ((bf16[32,64,256]{2,1,0:T(8,128)(2,1)}), bf16[32,64,256]{2,1,0:T(8,128)(2,1)S(1)}, u32[]{:S(2)}, u32[]{:S(2)}) async-start(bf16[32,64,256]{2,1,0:T(8,128)(2,1)} %bitcast.13), calls=%async_computation.1 | async-start | bytes 2097152 | tf_op jit(solution)/shard_map/all_to_all | solution.py:449
  206.9 1.0 copy-start.2
